TPU v7x, 512 devices: a whole 4x8x8 slice. The times are simulated.
512 devices in a mesh: batch: 16 (over z_lo, x, core), seq: 32 (over y, z_hi).
Axes of the slice: x: 4, y: 8, z: 8 (z_hi: 4, z_lo: 2; z = z_hi * 2 + z_lo), core: 2. Of those that a mesh axis runs over, the one named last changes fastest.
Arguments:
- layer_inputs: bfloat16 [409600, 800], P(('batch', 'seq')), may hold values from -24 to 24
- output_grads: bfloat16 [409600, 800], P(('batch', 'seq')), may hold values from -48 to 48
- input_inverse: float32 [800, 200], replicated, may hold values from -1 to 3
- output_inverse: float32 [800, 200], replicated, may hold values from -1 to 3
Outputs:
- input_factor: float32 [800, 200], P('seq')
- output_factor: float32 [800, 200], P('seq')
- preconditioned: bfloat16 [800, 800], replicated
All inputs are finite; a program needn't handle non-finite values.
Results may differ from a plain program's by a relative error of at most 0.0075.
Values may be sent and summed in bfloat16 or wider, within the bound.
A program may use at most 64 MiB of HBM per device.

v0:
```python
import jax
import jax.numpy as jnp
from jax import lax
from jax.sharding import Mesh
from jax.sharding import PartitionSpec as P

BLOCK = 200
SEQ = ("seq_0", "seq_1")
BATCH_SEQ = ("batch", "seq_0", "seq_1")


def scatter_axes(x, axes, dim):
    if not axes:
        return x
    nearer = lax.psum_scatter(x, axes[0], scatter_dimension=dim, tiled=True)
    return scatter_axes(nearer, axes[1:], dim)


def sent_to_all(x, axis):
    peers = lax.axis_size(axis)
    return lax.all_to_all(jnp.broadcast_to(x[None], (peers, *x.shape)), axis, 0, 0, tiled=True)


def taken_together(x, axis):
    return sent_to_all(x, axis).sum(axis=0)


def together(arrays, axis):
    ends = [0]
    for a in arrays:
        ends.append(ends[-1] + a.size)
    subtotal = taken_together(jnp.concatenate([a.ravel() for a in arrays]), axis)
    return tuple((subtotal[b:e].reshape(a.shape) for a, b, e in zip(arrays, ends, ends[1:])))


def block_terms(values):
    tok_rows, width = values.shape
    stacked = values.reshape(tok_rows, width // BLOCK, BLOCK)
    product = jnp.einsum("tnb,tnc->nbc", stacked, stacked, preferred_element_type=jnp.float32)
    return product.reshape(width, BLOCK)


def reduce_terms(input_term, output_term, grad_term):
    shares = (
        scatter_axes(input_term.astype(jnp.bfloat16), SEQ, 0).astype(jnp.float32),
        scatter_axes(output_term.astype(jnp.bfloat16), SEQ, 0).astype(jnp.float32),
        scatter_axes(grad_term.astype(jnp.bfloat16), SEQ, 0).astype(jnp.float32),
    )
    return together((shares[0], shares[1], shares[2]), "batch")


def shards(layer_inputs, output_grads, input_inverse, output_inverse):
    tok_rows, in_width = layer_inputs.shape
    out_width = output_grads.shape[1]
    in_blocks = in_width // BLOCK
    out_blocks = out_width // BLOCK
    total_rows = tok_rows * lax.axis_size("batch") * lax.axis_size(SEQ)
    inverse_count = 1.0 / total_rows
    input_term = block_terms(layer_inputs)
    output_term = block_terms(output_grads)
    input_stack = input_inverse.reshape(in_blocks, BLOCK, BLOCK)
    output_stack = output_inverse.reshape(out_blocks, BLOCK, BLOCK)
    grad_term = lax.dot_general(
        layer_inputs, output_grads, (((0,), (0,)), ((), ())), preferred_element_type=jnp.float32
    )
    input_sum, output_sum, grad_sum = reduce_terms(input_term, output_term, grad_term)
    grad_owned = grad_sum * inverse_count
    owned_rows = grad_owned.shape[0]
    right_done = jnp.einsum(
        "rmk,mkl->rml",
        grad_owned.reshape(owned_rows, out_blocks, BLOCK),
        output_stack,
        precision=lax.Precision.HIGHEST,
    ).reshape(owned_rows, out_width)
    gathered = lax.all_gather(right_done, SEQ, axis=0, tiled=True)
    applied = jnp.einsum(
        "nij,njo->nio",
        input_stack,
        gathered.reshape(in_blocks, BLOCK, out_width),
        precision=lax.Precision.HIGHEST,
    ).reshape(in_width, out_width)
    preconditioned = applied.astype(jnp.bfloat16)
    input_factor = input_sum * inverse_count
    output_factor = output_sum * inverse_count
    return (input_factor, output_factor, preconditioned)


def solution(mesh):
    finer = Mesh(mesh.devices.reshape(mesh.shape["batch"], 8, 4), ("batch", "seq_0", "seq_1"))
    in_specs = (P(BATCH_SEQ, None), P(BATCH_SEQ, None), P(), P())
    out_specs = (P(SEQ, None), P(SEQ, None), P())
    return jax.shard_map(
        shards, mesh=finer, in_specs=in_specs, out_specs=out_specs, check_vma=False
    )
```

profile of v0, /device:TPU:2, one launch (start us, length us, event | category | flops | bytes accessed | tf_op | source)
XLA Modules:
  0.0 250.9 jit_solution(5033083344006876032)
XLA Ops:
  7.2 2.8 %copy.31 = bf16[800,800]{0,1:T(8,128)(2,1)S(1)} copy(bf16[800,800]{1,0:T(8,128)(2,1)} %param.4) | data formatting | bytes 2560000 | tf_op args[0]
  9.9 2.8 %copy.32 = bf16[800,800]{0,1:T(8,128)(2,1)S(1)} copy(bf16[800,800]{1,0:T(8,128)(2,1)} %param.5) | data formatting | bytes 2560000 | tf_op args[1]
  12.7 4.8 %convolution_convert_fusion.1 = bf16[800,800]{1,0:T(8,128)(2,1)} fusion(bf16[800,800]{1,0:T(8,128)(2,1)} %param.4, bf16[800,800]{1,0:T(8,128)(2,1)} %param.5), kind=kOutput, calls=%fused_computation.1 | convolution fusion | flops 1024640000 | bytes 3840000 | tf_op jit(solution)/shard_map/dot_general | solution.py:63
  18.7 34.1 %fusion.7 = (bf16[104,200]{1,0:T(8,128)(2,1)S(1)}, bf16[104,200]{1,0:T(8,128)(2,1)S(1)}, bf16[112,800]{1,0:T(8,128)(2,1)S(1)}) fusion(bf16[800,200]{1,0:T(8,128)(2,1)S(1)} %bitcast.40, bf16[800,200]{1,0:T(8,128)(2,1)S(1)} %bitcast.41, bf16[800,800]{1,0:T(8,128)(2,1)} %convolution_convert_fusion.1), kind=kCustom, calls=%all-reduce-scatter.6 | all-reduce-scatter fusion | flops 1049602 | bytes 2184448
  52.8 2.6 %collective-permute-start = (bf16[28,200]{1,0:T(8,128)(2,1)S(1)}, bf16[28,200]{1,0:T(8,128)(2,1)S(1)}, u32[]{:S(2)}, u32[]{:S(2)}) collective-permute-start(bf16[28,200]{1,0:T(8,128)(2,1)S(1)} %slice.31), channel_id=1, source_target_pairs={{0,4},{4,8},{8,12},{12,16},{16,20},{20,24},{24,28},{1,5},{5,9},{9,... | collective-permute-start | bytes 33608
  55.4 1.9 collective-permute-start.2
  57.4 3.4 %collective-permute-start.4 = (bf16[84,800]{1,0:T(8,128)(2,1)S(1)}, bf16[84,800]{1,0:T(8,128)(2,1)S(1)}, u32[]{:S(2)}, u32[]{:S(2)}) collective-permute-start(bf16[84,800]{1,0:T(8,128)(2,1)S(1)} %slice.35), channel_id=1, source_target_pairs={{0,4},{4,8},{8,12},{12,16},{16,20},{20,24},{24,28},{1,5},{5,9},{9,... | collective-permute-start | bytes 403208
  60.8 1.3 dynamic-slice.14
  64.6 21.1 %fusion.8 = (bf16[32,200]{1,0:T(8,128)(2,1)S(1)}, bf16[32,200]{1,0:T(8,128)(2,1)S(1)}, bf16[32,800]{1,0:T(8,128)(2,1)S(1)}) fusion(bf16[100,200]{1,0:T(8,128)(2,1)S(1)} %constant_dynamic-slice_fusion.5, bf16[100,200]{1,0:T(8,128)(2,1)S(1)} %constant_dynamic-slice_fusion.3, bf16[100,800]{1,0:T(8,128)(2,1)S(1)} %constant_dynamic-slice_fusion.1), kind=kCustom, calls=%all-reduce-scatter.7 | all-reduce-scatter fusion | flops 153601 | bytes 318848
  85.8 1.5 collective-permute-start.1
  87.3 1.3 dynamic-slice.18
  89.3 5.6 %collective-permute-start.3 = (bf16[21,200]{1,0:T(8,128)(2,1)S(1)}, bf16[21,200]{1,0:T(8,128)(2,1)S(1)}, u32[]{:S(2)}, u32[]{:S(2)}) collective-permute-start(bf16[21,200]{1,0:T(8,128)(2,1)S(1)} %slice.34), channel_id=1, source_target_pairs={{0,1},{1,2},{2,3},{4,5},{5,6},{6,7},{8,9},{9,10},{10,11},{12,13},{... | collective-permute-start | bytes 25208
  94.9 3.3 %collective-permute-start.5 = (bf16[21,800]{1,0:T(8,128)(2,1)S(1)}, bf16[21,800]{1,0:T(8,128)(2,1)S(1)}, u32[]{:S(2)}, u32[]{:S(2)}) collective-permute-start(bf16[21,800]{1,0:T(8,128)(2,1)S(1)} %slice.36), channel_id=1, source_target_pairs={{0,1},{1,2},{2,3},{4,5},{5,6},{6,7},{8,9},{9,10},{10,11},{12,13},{... | collective-permute-start | bytes 100808
  98.9 1.0 collective-permute-done.5
  100.5 2.3 broadcast_in_dim.2
  102.7 5.5 %all-to-all-start = ((f32[16,1,30000]{2,1,0:T(1,128)}), f32[16,1,30000]{2,1,0:T(1,128)S(1)}, u32[]{:S(2)}, u32[]{:S(2)}) async-start(f32[16,1,30000]{2,1,0:T(1,128)} %broadcast_in_dim.2), calls=%async_computation | async-start | bytes 3850240 | tf_op jit(solution)/shard_map/all_to_all | solution.py:21
  108.7 24.1 %all-to-all-done = f32[16,1,30000]{2,1,0:T(1,128)S(1)} async-done(((f32[16,1,30000]{2,1,0:T(1,128)}), f32[16,1,30000]{2,1,0:T(1,128)S(1)}, u32[]{:S(2)}, u32[]{:S(2)}) %all-to-all-start) | async-done | bytes 1920032 | tf_op jit(solution)/shard_map/all_to_all | solution.py:21
  132.8 1.2 reduce_sum.9
  135.0 0.8 reshape.84
  135.8 1.2 copy.39
  137.0 0.7 mul.23
  138.5 98.1 %all-gather.3.cloned.1.call-done = f32[32,25,800]{2,1,0:T(8,128)} async-done(((f32[1,25,800]{2,1,0:T(8,128)}), f32[32,25,800]{2,1,0:T(8,128)}) %all-gather.3.cloned.1.call-update) | async-done | bytes 2560016 | tf_op jit(solution)/shard_map/all_gather | solution.py:75
  236.5 2.2 reshape.82
  238.8 5.3 %convolution_convert_fusion = bf16[4,800,200]{1,2,0:T(8,128)(2,1)} fusion(f32[4,200,800]{2,1,0:T(8,128)S(1)} %reshape.82, f32[4,200,200]{2,1,0:T(8,128)} %bitcast.38), kind=kOutput, calls=%fused_computation | convolution fusion | flops 1536640000 | bytes 4480000 | tf_op jit(solution)/shard_map/nij,njo->nio/dot_general | solution.py:76
  (42 shorter events, 5.9 us)
Async XLA Ops:
  52.8 10.6 %collective-permute-start = (bf16[28,200]{1,0:T(8,128)(2,1)S(1)}, bf16[28,200]{1,0:T(8,128)(2,1)S(1)}, u32[]{:S(2)}, u32[]{:S(2)}) collective-permute-start(bf16[28,200]{1,0:T(8,128)(2,1)S(1)} %slice.31), channel_id=1, source_target_pairs={{0,4},{4,8},{8,12},{12,16},{16,20},{20,24},{24,28},{1,5},{5,9},{9,... | collective-permute-start | bytes 33608
  55.4 8.2 %collective-permute-start.2 = (bf16[28,200]{1,0:T(8,128)(2,1)S(1)}, bf16[28,200]{1,0:T(8,128)(2,1)S(1)}, u32[]{:S(2)}, u32[]{:S(2)}) collective-permute-start(bf16[28,200]{1,0:T(8,128)(2,1)S(1)} %slice.33), channel_id=1, source_target_pairs={{0,4},{4,8},{8,12},{12,16},{16,20},{20,24},{24,28},{1,5},{5,9},{9,... | collective-permute-start | bytes 33608
  57.4 6.5 %collective-permute-start.4 = (bf16[84,800]{1,0:T(8,128)(2,1)S(1)}, bf16[84,800]{1,0:T(8,128)(2,1)S(1)}, u32[]{:S(2)}, u32[]{:S(2)}) collective-permute-start(bf16[84,800]{1,0:T(8,128)(2,1)S(1)} %slice.35), channel_id=1, source_target_pairs={{0,4},{4,8},{8,12},{12,16},{16,20},{20,24},{24,28},{1,5},{5,9},{9,... | collective-permute-start | bytes 403208
  85.8 12.4 %collective-permute-start.1 = (bf16[21,200]{1,0:T(8,128)(2,1)S(1)}, bf16[21,200]{1,0:T(8,128)(2,1)S(1)}, u32[]{:S(2)}, u32[]{:S(2)}) collective-permute-start(bf16[21,200]{1,0:T(8,128)(2,1)S(1)} %slice.32), channel_id=1, source_target_pairs={{0,1},{1,2},{2,3},{4,5},{5,6},{6,7},{8,9},{9,10},{10,11},{12,13},{... | collective-permute-start | bytes 25208
  89.3 9.1 %collective-permute-start.3 = (bf16[21,200]{1,0:T(8,128)(2,1)S(1)}, bf16[21,200]{1,0:T(8,128)(2,1)S(1)}, u32[]{:S(2)}, u32[]{:S(2)}) collective-permute-start(bf16[21,200]{1,0:T(8,128)(2,1)S(1)} %slice.34), channel_id=1, source_target_pairs={{0,1},{1,2},{2,3},{4,5},{5,6},{6,7},{8,9},{9,10},{10,11},{12,13},{... | collective-permute-start | bytes 25208
  94.9 5.0 %collective-permute-start.5 = (bf16[21,800]{1,0:T(8,128)(2,1)S(1)}, bf16[21,800]{1,0:T(8,128)(2,1)S(1)}, u32[]{:S(2)}, u32[]{:S(2)}) collective-permute-start(bf16[21,800]{1,0:T(8,128)(2,1)S(1)} %slice.36), channel_id=1, source_target_pairs={{0,1},{1,2},{2,3},{4,5},{5,6},{6,7},{8,9},{9,10},{10,11},{12,13},{... | collective-permute-start | bytes 100808
  102.7 5.7 %copy-start = (f32[800,200]{0,1:T(8,128)S(1)}, f32[800,200]{0,1:T(8,128)}, u32[]{:S(2)}) copy-start(f32[800,200]{0,1:T(8,128)} %param.7) | copy-start | bytes 1920004
  102.7 30.1 %all-to-all-start = ((f32[16,1,30000]{2,1,0:T(1,128)}), f32[16,1,30000]{2,1,0:T(1,128)S(1)}, u32[]{:S(2)}, u32[]{:S(2)}) async-start(f32[16,1,30000]{2,1,0:T(1,128)} %broadcast_in_dim.2), calls=%async_computation | async-start | bytes 3850240 | tf_op jit(solution)/shard_map/all_to_all | solution.py:21
  108.2 128.3 %all-gather.3.cloned.1.call-start = ((), (), s32[]{:S(2)}) async-start(), calls=%async_computation.1 | async-start | bytes 3784704 | tf_op jit(solution)/shard_map/all_gather | solution.py:75
  134.0 1.8 copy-start.1
Sparse Core Ops, SparseCore 0:
  135.9 100.5 all-gather.2
where the time goes:
time: 251 us
  waiting for transfers between devices  123 us (49%)
  blocking collectives  55.2 us (22%)
  starting transfers between devices  24 us (10%)
  local copies, waits for them, and re-layouts  18.9 us (8%)
  between operations  16.4 us (7%)
  matrix products  11.8 us (5%)
    all_gather x1, waiting for transfers between devices, shards(): gathered = lax.all_gather(right_done, SEQ, axis=0, tiled=True)  98.1 us
    unnamed x2, blocking collectives  55.2 us
    all_to_all x1, waiting for transfers between devices, sent_to_all(): lax.all_to_all(jnp.broadcast_to(x[None], (peers, *x.shape)), axis, 0, 0,...  24.1 us
    unnamed x6, starting transfers between devices  18.3 us
    unnamed x27, local copies, waits for them, and re-layouts  10.8 us
    all_to_all x1, starting transfers between devices, sent_to_all(): lax.all_to_all(jnp.broadcast_to(x[None], (peers, *x.shape)), axis, 0, 0,...  5.46 us
    dot_general x1, matrix products, shards(): jnp.einsum('nij,njo->nio', input_stack, gathered.reshape(in_blocks, BLOCK...  5.26 us
  transfers between devices with their start and end apart: 8, of which 3 were waited for; matrix products, arithmetic and copies ran while one was open for 3% of the time, Pallas kernels for 0%

commit v1 on v0

--- a/solution.py
+++ b/solution.py
@@ -72,7 +72,8 @@
         output_stack,
         precision=lax.Precision.HIGHEST,
     ).reshape(owned_rows, out_width)
-    gathered = lax.all_gather(right_done, SEQ, axis=0, tiled=True)
+    sent = jnp.stack([right_done] * lax.axis_size(SEQ))
+    gathered = jnp.concatenate(lax.all_to_all(sent, SEQ, 0, 0), axis=0)
     applied = jnp.einsum(
         "nij,njo->nio",
         input_stack,

time: 251 us -> 273 us (1.088)
  the two profiles are of different devices: /device:TPU:2 before, /device:TPU:350 now
where the time goes in v1:
time: 273 us
  waiting for transfers between devices  155 us (57%)
  blocking collectives  46.6 us (17%)
  starting transfers between devices  34.7 us (13%)
  local copies, waits for them, and re-layouts  20.4 us (7%)
  matrix products  11.8 us (4%)
  between operations  2.94 us (1%)
    all_to_all x1, waiting for transfers between devices, shards(): gathered = jnp.concatenate(lax.all_to_all(sent, SEQ, 0, 0), axis=0)  122 us
    unnamed x2, blocking collectives  46.6 us
    all_to_all x1, waiting for transfers between devices, sent_to_all(): lax.all_to_all(jnp.broadcast_to(x[None], (peers, *x.shape)), axis, 0, 0,...  25.6 us
    unnamed x6, starting transfers between devices  17 us
    all_to_all x1, starting transfers between devices, shards(): gathered = jnp.concatenate(lax.all_to_all(sent, SEQ, 0, 0), axis=0)  11.9 us
    unnamed x26, local copies, waits for them, and re-layouts  9.94 us
    unnamed x6, waiting for transfers between devices  7.14 us
    all_to_all x1, starting transfers between devices, sent_to_all(): lax.all_to_all(jnp.broadcast_to(x[None], (peers, *x.shape)), axis, 0, 0,...  5.81 us
  transfers between devices with their start and end apart: 8, of which 5 were waited for; matrix products, arithmetic and copies ran while one was open for 2% of the time, Pallas kernels for 0%

profile of v1, /device:TPU:350, one launch (start us, length us, event | category | flops | bytes accessed | tf_op | source)
XLA Modules:
  0.0 272.6 jit_solution(17172507324947263709)
XLA Ops:
  0.6 2.8 %copy.31 = bf16[800,800]{0,1:T(8,128)(2,1)S(1)} copy(bf16[800,800]{1,0:T(8,128)(2,1)} %param.4) | data formatting | bytes 2560000 | tf_op args[0]
  3.4 2.8 %copy.32 = bf16[800,800]{0,1:T(8,128)(2,1)S(1)} copy(bf16[800,800]{1,0:T(8,128)(2,1)} %param.5) | data formatting | bytes 2560000 | tf_op args[1]
  6.1 4.8 %convolution_convert_fusion.1 = bf16[800,800]{1,0:T(8,128)(2,1)} fusion(bf16[800,800]{1,0:T(8,128)(2,1)} %param.4, bf16[800,800]{1,0:T(8,128)(2,1)} %param.5), kind=kOutput, calls=%fused_computation.1 | convolution fusion | flops 1024640000 | bytes 3840000 | tf_op jit(solution)/shard_map/dot_general | solution.py:63
  12.2 31.6 %fusion.7 = (bf16[104,200]{1,0:T(8,128)(2,1)S(1)}, bf16[104,200]{1,0:T(8,128)(2,1)S(1)}, bf16[112,800]{1,0:T(8,128)(2,1)S(1)}) fusion(bf16[800,200]{1,0:T(8,128)(2,1)S(1)} %bitcast.40, bf16[800,200]{1,0:T(8,128)(2,1)S(1)} %bitcast.41, bf16[800,800]{1,0:T(8,128)(2,1)} %convolution_convert_fusion.1), kind=kCustom, calls=%all-reduce-scatter.6 | all-reduce-scatter fusion | flops 1049602 | bytes 2184448
  43.7 5.6 %collective-permute-start = (bf16[28,200]{1,0:T(8,128)(2,1)S(1)}, bf16[28,200]{1,0:T(8,128)(2,1)S(1)}, u32[]{:S(2)}, u32[]{:S(2)}) collective-permute-start(bf16[28,200]{1,0:T(8,128)(2,1)S(1)} %slice.31), channel_id=1, source_target_pairs={{0,4},{4,8},{8,12},{12,16},{16,20},{20,24},{24,28},{1,5},{5,9},{9,... | collective-permute-start | bytes 33608
  49.4 1.9 collective-permute-start.2
  51.3 2.8 %collective-permute-start.4 = (bf16[84,800]{1,0:T(8,128)(2,1)S(1)}, bf16[84,800]{1,0:T(8,128)(2,1)S(1)}, u32[]{:S(2)}, u32[]{:S(2)}) collective-permute-start(bf16[84,800]{1,0:T(8,128)(2,1)S(1)} %slice.35), channel_id=1, source_target_pairs={{0,4},{4,8},{8,12},{12,16},{16,20},{20,24},{24,28},{1,5},{5,9},{9,... | collective-permute-start | bytes 403208
  54.1 1.3 dynamic-slice.14
  57.2 1.3 collective-permute-done.4
  59.2 15.1 %fusion.8 = (bf16[32,200]{1,0:T(8,128)(2,1)S(1)}, bf16[32,200]{1,0:T(8,128)(2,1)S(1)}, bf16[32,800]{1,0:T(8,128)(2,1)S(1)}) fusion(bf16[100,200]{1,0:T(8,128)(2,1)S(1)} %constant_dynamic-slice_fusion.5, bf16[100,200]{1,0:T(8,128)(2,1)S(1)} %constant_dynamic-slice_fusion.3, bf16[100,800]{1,0:T(8,128)(2,1)S(1)} %constant_dynamic-slice_fusion.1), kind=kCustom, calls=%all-reduce-scatter.7 | all-reduce-scatter fusion | flops 153601 | bytes 318848
  74.3 2.9 %collective-permute-start.1 = (bf16[21,200]{1,0:T(8,128)(2,1)S(1)}, bf16[21,200]{1,0:T(8,128)(2,1)S(1)}, u32[]{:S(2)}, u32[]{:S(2)}) collective-permute-start(bf16[21,200]{1,0:T(8,128)(2,1)S(1)} %slice.32), channel_id=1, source_target_pairs={{0,1},{1,2},{2,3},{4,5},{5,6},{6,7},{8,9},{9,10},{10,11},{12,13},{... | collective-permute-start | bytes 25208
  77.2 1.3 dynamic-slice.18
  79.1 1.9 collective-permute-start.3
  81.1 1.9 collective-permute-start.5
  83.2 3.6 %collective-permute-done.3 = bf16[21,200]{1,0:T(8,128)(2,1)S(1)} collective-permute-done((bf16[21,200]{1,0:T(8,128)(2,1)S(1)}, bf16[21,200]{1,0:T(8,128)(2,1)S(1)}, u32[]{:S(2)}, u32[]{:S(2)}) %collective-permute-start.3) | collective-permute-done | bytes 8432
  87.2 2.2 collective-permute-done.5
  90.0 2.3 broadcast_in_dim.2
  92.3 5.8 %all-to-all-start = ((f32[16,1,30000]{2,1,0:T(1,128)}), f32[16,1,30000]{2,1,0:T(1,128)S(1)}, u32[]{:S(2)}, u32[]{:S(2)}) async-start(f32[16,1,30000]{2,1,0:T(1,128)} %broadcast_in_dim.2), calls=%async_computation | async-start | bytes 3850240 | tf_op jit(solution)/shard_map/all_to_all | solution.py:21
  98.4 25.6 %all-to-all-done = f32[16,1,30000]{2,1,0:T(1,128)S(1)} async-done(((f32[16,1,30000]{2,1,0:T(1,128)}), f32[16,1,30000]{2,1,0:T(1,128)S(1)}, u32[]{:S(2)}, u32[]{:S(2)}) %all-to-all-start) | async-done | bytes 1920032 | tf_op jit(solution)/shard_map/all_to_all | solution.py:21
  126.3 2.3 stack.3
  128.5 11.9 %all-to-all-start.1 = ((f32[32,25,800]{2,1,0:T(8,128)}), f32[32,25,800]{2,1,0:T(8,128)}, u32[]{:S(2)}, u32[]{:S(2)}) async-start(f32[32,25,800]{2,1,0:T(8,128)} %stack.3), calls=%async_computation.1 | async-start | bytes 7340032 | tf_op jit(solution)/shard_map/all_to_all | solution.py:76
  143.1 122.0 %all-to-all-done.1 = f32[32,25,800]{2,1,0:T(8,128)} async-done(((f32[32,25,800]{2,1,0:T(8,128)}), f32[32,25,800]{2,1,0:T(8,128)}, u32[]{:S(2)}, u32[]{:S(2)}) %all-to-all-start.1) | async-done | bytes 2560032 | tf_op jit(solution)/shard_map/all_to_all | solution.py:76
  265.1 2.2 reshape_reshape.3
  267.4 5.3 %convolution_convert_fusion = bf16[4,800,200]{1,2,0:T(8,128)(2,1)} fusion(f32[4,200,800]{2,1,0:T(8,128)S(1)} %reshape_reshape.3, f32[4,200,200]{2,1,0:T(8,128)} %bitcast.38), kind=kOutput, calls=%fused_computation | convolution fusion | flops 1536640000 | bytes 4480000 | tf_op jit(solution)/shard_map/nij,njo->nio/dot_general | solution.py:77
  (42 shorter events, 8.8 us)
Async XLA Ops:
  43.7 12.9 %collective-permute-start = (bf16[28,200]{1,0:T(8,128)(2,1)S(1)}, bf16[28,200]{1,0:T(8,128)(2,1)S(1)}, u32[]{:S(2)}, u32[]{:S(2)}) collective-permute-start(bf16[28,200]{1,0:T(8,128)(2,1)S(1)} %slice.31), channel_id=1, source_target_pairs={{0,4},{4,8},{8,12},{12,16},{16,20},{20,24},{24,28},{1,5},{5,9},{9,... | collective-permute-start | bytes 33608
  49.4 7.6 %collective-permute-start.2 = (bf16[28,200]{1,0:T(8,128)(2,1)S(1)}, bf16[28,200]{1,0:T(8,128)(2,1)S(1)}, u32[]{:S(2)}, u32[]{:S(2)}) collective-permute-start(bf16[28,200]{1,0:T(8,128)(2,1)S(1)} %slice.33), channel_id=1, source_target_pairs={{0,4},{4,8},{8,12},{12,16},{16,20},{20,24},{24,28},{1,5},{5,9},{9,... | collective-permute-start | bytes 33608
  51.3 7.1 %collective-permute-start.4 = (bf16[84,800]{1,0:T(8,128)(2,1)S(1)}, bf16[84,800]{1,0:T(8,128)(2,1)S(1)}, u32[]{:S(2)}, u32[]{:S(2)}) collective-permute-start(bf16[84,800]{1,0:T(8,128)(2,1)S(1)} %slice.35), channel_id=1, source_target_pairs={{0,4},{4,8},{8,12},{12,16},{16,20},{20,24},{24,28},{1,5},{5,9},{9,... | collective-permute-start | bytes 403208
  74.3 8.7 %collective-permute-start.1 = (bf16[21,200]{1,0:T(8,128)(2,1)S(1)}, bf16[21,200]{1,0:T(8,128)(2,1)S(1)}, u32[]{:S(2)}, u32[]{:S(2)}) collective-permute-start(bf16[21,200]{1,0:T(8,128)(2,1)S(1)} %slice.32), channel_id=1, source_target_pairs={{0,1},{1,2},{2,3},{4,5},{5,6},{6,7},{8,9},{9,10},{10,11},{12,13},{... | collective-permute-start | bytes 25208
  79.1 7.7 %collective-permute-start.3 = (bf16[21,200]{1,0:T(8,128)(2,1)S(1)}, bf16[21,200]{1,0:T(8,128)(2,1)S(1)}, u32[]{:S(2)}, u32[]{:S(2)}) collective-permute-start(bf16[21,200]{1,0:T(8,128)(2,1)S(1)} %slice.34), channel_id=1, source_target_pairs={{0,1},{1,2},{2,3},{4,5},{5,6},{6,7},{8,9},{9,10},{10,11},{12,13},{... | collective-permute-start | bytes 25208
  81.1 8.4 %collective-permute-start.5 = (bf16[21,800]{1,0:T(8,128)(2,1)S(1)}, bf16[21,800]{1,0:T(8,128)(2,1)S(1)}, u32[]{:S(2)}, u32[]{:S(2)}) collective-permute-start(bf16[21,800]{1,0:T(8,128)(2,1)S(1)} %slice.36), channel_id=1, source_target_pairs={{0,1},{1,2},{2,3},{4,5},{5,6},{6,7},{8,9},{9,10},{10,11},{12,13},{... | collective-permute-start | bytes 100808
  92.3 5.8 %copy-start = (f32[800,200]{0,1:T(8,128)S(1)}, f32[800,200]{0,1:T(8,128)}, u32[]{:S(2)}) copy-start(f32[800,200]{0,1:T(8,128)} %param.7) | copy-start | bytes 1920004
  92.3 31.7 %all-to-all-start = ((f32[16,1,30000]{2,1,0:T(1,128)}), f32[16,1,30000]{2,1,0:T(1,128)S(1)}, u32[]{:S(2)}, u32[]{:S(2)}) async-start(f32[16,1,30000]{2,1,0:T(1,128)} %broadcast_in_dim.2), calls=%async_computation | async-start | bytes 3850240 | tf_op jit(solution)/shard_map/all_to_all | solution.py:21
  128.5 11.9 %copy-start.1 = (f32[800,200]{0,1:T(8,128)S(1)}, f32[800,200]{0,1:T(8,128)}, u32[]{:S(2)}) copy-start(f32[800,200]{0,1:T(8,128)} %param.6) | copy-start | bytes 1920004
  128.5 136.6 %all-to-all-start.1 = ((f32[32,25,800]{2,1,0:T(8,128)}), f32[32,25,800]{2,1,0:T(8,128)}, u32[]{:S(2)}, u32[]{:S(2)}) async-start(f32[32,25,800]{2,1,0:T(8,128)} %stack.3), calls=%async_computation.1 | async-start | bytes 7340032 | tf_op jit(solution)/shard_map/all_to_all | solution.py:76
